TPU v7x, 32 devices: a whole 2x2x4 slice. The times are simulated.
32 devices in a mesh: fsdp: 8 (over z, x), rep: 4 (over y, core).
Axes of the slice: x: 2, y: 2, z: 4, core: 2. Of those that a mesh axis runs over, the one named last changes fastest.
Arguments:
- partials: bfloat16 [4, 56, 1024, 1024], P('rep', None, 'fsdp'), may hold values from -400 to 400
- sketch: bfloat16 [8, 4, 2, 1024, 256], P('fsdp', 'rep'), may hold values from -3 to 3
- owner_table: int32 [56, 1], replicated, may hold values from 0 to 7; in each aligned block of 14 rows (0 to 13, 14 to 27, ...) at most 2 rows name the same one
Outputs:
- update: bfloat16 [56, 1024, 1024], P('rep', 'fsdp')
- new_sketch: bfloat16 [8, 4, 2, 1024, 256], P('fsdp', 'rep')
Inputs may be any that keep to these rules, and one draw needn't show every extreme that they name: `owner_table`: in each aligned slice of 14 blocks no owner holds more than 2 blocks; some owner holds exactly 2 in some slice.
All inputs are finite; a program needn't handle non-finite values.
Results may differ from a plain program's by a relative error of at most 0.015.
Values may be sent and summed in bfloat16 or wider, within the bound.
No kernel may reach another device: no remote copies, remote signals or barrier semaphores. Data moves between devices by JAX's collectives and lax.ppermute only.
A program may use at most 128 MiB of HBM per device.

v0:
```python
import math
import jax
import jax.numpy as jnp
from jax import lax
from jax.sharding import PartitionSpec as P

NS_ITERS = 5
DECAY = 0.9
DAMPING = 64.0
FIRST_AXES = (((0,), (0,)), ((), ()))
LAST_AXES = (((1,), (1,)), ((), ()))


def inverse_root(matrix, epsilon):
    identity = jnp.eye(matrix.shape[0], dtype=jnp.float32)
    trace_sum = jnp.trace(matrix) + epsilon
    current = matrix / trace_sum
    inverse = identity
    for repeat in range(NS_ITERS):
        middle = 1.5 * identity - 0.5 * jnp.dot(inverse, current, precision=lax.Precision.HIGHEST)
        current = jnp.dot(current, middle, precision=lax.Precision.HIGHEST)
        inverse = jnp.dot(middle, inverse, precision=lax.Precision.HIGHEST)
    return inverse / jnp.sqrt(trace_sum)


def precondition(gradient, current_sketch):
    identity = jnp.eye(current_sketch.shape[1], dtype=jnp.float32)
    projected = lax.dot_general(
        gradient, current_sketch, FIRST_AXES, preferred_element_type=jnp.float32
    ).astype(jnp.bfloat16)
    gram_matrix = lax.dot_general(
        current_sketch, current_sketch, FIRST_AXES, preferred_element_type=jnp.float32
    ).astype(jnp.bfloat16)
    powered = DECAY * jnp.dot(
        current_sketch, gram_matrix, preferred_element_type=jnp.float32
    ) + jnp.dot(gradient, projected, preferred_element_type=jnp.float32)
    inner_gram = lax.dot_general(powered, powered, FIRST_AXES, precision=lax.Precision.HIGHEST)
    basis_full = jnp.dot(powered, inverse_root(inner_gram, 1e-06), precision=lax.Precision.HIGHEST)
    basis_low = basis_full.astype(jnp.bfloat16)
    coefficients = lax.dot_general(
        gradient, basis_low, FIRST_AXES, preferred_element_type=jnp.float32
    ).astype(jnp.bfloat16)
    alignment = lax.dot_general(
        current_sketch, basis_low, FIRST_AXES, preferred_element_type=jnp.float32
    )
    energy = DECAY * lax.dot_general(
        alignment, alignment, FIRST_AXES, precision=lax.Precision.HIGHEST
    ) + lax.dot_general(coefficients, coefficients, FIRST_AXES, preferred_element_type=jnp.float32)
    root_inverse = inverse_root(energy + DAMPING * identity, 0.0)
    inner_part = jnp.dot(energy, root_inverse, precision=lax.Precision.HIGHEST)
    new_block = jnp.dot(basis_full, inner_part, precision=lax.Precision.HIGHEST).astype(
        jnp.bfloat16
    )
    mix_matrix = math.sqrt(DAMPING) * root_inverse - identity
    side_terms = lax.dot_general(
        coefficients.astype(jnp.float32), mix_matrix, LAST_AXES, precision=lax.Precision.HIGHEST
    ).astype(jnp.bfloat16)
    update_block = (
        gradient.astype(jnp.float32)
        + lax.dot_general(basis_low, side_terms, LAST_AXES, preferred_element_type=jnp.float32)
    ).astype(jnp.bfloat16)
    return (update_block, new_block)


def squared_sum(values):
    wide = values.astype(jnp.float32)
    return jnp.sum(wide * wide)


def process_slot(slot_index, arrived, clip_factor, held_sketches, filled):
    block_width = arrived.shape[-1]
    gradient = (clip_factor * arrived.reshape(block_width, block_width).astype(jnp.float32)).astype(
        jnp.bfloat16
    )
    current_sketch = held_sketches[slot_index]
    active = slot_index < filled
    update_block, new_block = precondition(gradient, current_sketch)
    new_block = jnp.where(active, new_block, current_sketch)
    return (update_block, new_block)


def local(partials, sketch, owner_table):
    block_total = partials.shape[1]
    row_count = partials.shape[2]
    block_width = partials.shape[3]
    fsdp_count = lax.axis_size("fsdp")
    per_slice = block_total // lax.axis_size("rep")
    slot_count = sketch.shape[2]
    reduced = lax.psum_scatter(
        partials[0].astype(jnp.float32).astype(jnp.bfloat16), "rep", scatter_dimension=0, tiled=True
    )
    my_owners = lax.dynamic_slice_in_dim(
        owner_table[:, 0], lax.axis_index("rep") * per_slice, per_slice
    )
    positions = jnp.arange(per_slice, dtype=jnp.int32)
    same_owner = (my_owners[:, None] == my_owners[None, :]) & (
        positions[:, None] < positions[None, :]
    )
    rank_in = jnp.sum(same_owner.astype(jnp.int32), axis=0)
    target = rank_in * fsdp_count + my_owners
    selector = (
        target[None, :] == jnp.arange(slot_count * fsdp_count, dtype=jnp.int32)[:, None]
    ).astype(jnp.bfloat16)
    flattened = reduced.reshape(per_slice, row_count * block_width)
    outgoing = jnp.dot(selector, flattened, preferred_element_type=jnp.float32).astype(jnp.bfloat16)
    outgoing = outgoing.reshape(slot_count, fsdp_count, row_count, block_width)
    sum_squares = lax.psum(squared_sum(reduced), ("fsdp", "rep"))
    clip_limit = 0.5 * math.sqrt(block_total * block_width * block_width)
    clip_factor = jnp.minimum(1.0, clip_limit / jnp.sqrt(sum_squares + 1e-06))
    filled = jnp.sum((my_owners == lax.axis_index("fsdp")).astype(jnp.int32))
    held_sketches = sketch[0, 0]
    fresh_list = []
    incoming = lax.all_to_all(outgoing, "fsdp", split_axis=1, concat_axis=1, tiled=True)
    update_list = []
    for slot_index in range(slot_count):
        update_block, new_block = process_slot(
            slot_index, incoming[slot_index], clip_factor, held_sketches, filled
        )
        update_list.append(update_block)
        fresh_list.append(new_block)
    stacked = jnp.stack(update_list).reshape(slot_count, fsdp_count, row_count, block_width)
    returned = lax.all_to_all(stacked, "fsdp", split_axis=1, concat_axis=1, tiled=True)
    returned = returned.reshape(slot_count * fsdp_count, row_count * block_width)
    my_updates = lax.dot_general(
        selector, returned, FIRST_AXES, preferred_element_type=jnp.float32
    ).astype(jnp.bfloat16)
    my_updates = my_updates.reshape(per_slice, row_count, block_width)
    return (my_updates, jnp.stack(fresh_list)[None, None])


def solution(mesh):
    placed = (P("rep", None, "fsdp", None), P("fsdp", "rep", None, None, None), P())
    return jax.shard_map(
        local,
        mesh=mesh,
        in_specs=placed,
        out_specs=(P("rep", "fsdp", None), P("fsdp", "rep", None, None, None)),
        check_vma=False,
    )
```

profile of v0, /device:TPU:0, one launch (start us, length us, event | category | flops | bytes accessed | tf_op | source)
XLA Modules:
  0.0 441.0 jit_solution(7717073570326933660)
XLA Ops:
  8.8 118.5 %reduce-scatter.2.cloned.1.call-done = bf16[14,128,1024]{2,1,0:T(8,128)(2,1)} async-done(((bf16[56,128,1024]{2,1,0:T(8,128)(2,1)}), bf16[14,128,1024]{2,1,0:T(8,128)(2,1)}) %reduce-scatter.2.cloned.1.call-update) | async-done | bytes 3670032 | tf_op jit(solution)/shard_map/reduce_scatter | solution.py:89
  127.3 2.5 pad.4
  129.8 2.3 copy.28
  132.1 1.2 convolution_convert_fusion.1
  133.3 4.3 copy.20
  137.6 5.5 %all-to-all-start = ((bf16[2,8,128,1024]{3,2,0,1:T(8,128)(2,1)}), bf16[2,8,128,1024]{3,2,0,1:T(8,128)(2,1)}, u32[]{:S(2)}, u32[]{:S(2)}) async-start(bf16[2,8,128,1024]{3,2,0,1:T(8,128)(2,1)} %copy.20), calls=%async_computation.1 | async-start | bytes 8388608 | tf_op jit(solution)/shard_map/all_to_all | solution.py:113
  143.1 4.5 %multiply_reduce_fusion = f32[]{:T(128)} fusion(bf16[14,128,1024]{2,1,0:T(8,128)(2,1)} %reduce-scatter.2.cloned.1.call-done), kind=kLoop, calls=%fused_computation.2 | loop fusion | flops 5505023 | bytes 3670020 | tf_op jit(solution)/shard_map/reduce_sum | solution.py:67
  147.7 108.8 %psum.7 = f32[]{:T(128)} all-reduce(f32[]{:T(128)} %multiply_reduce_fusion), channel_id=1, replica_groups=mesh['fsdp'=8,'rep'=4] {'fsdp','rep'}, use_global_device_ids=true, to_apply=%region_3.0 | all-reduce | flops 1 | bytes 8 | tf_op jit(solution)/shard_map/psum | solution.py:107
  257.2 4.9 %multiply_convert_fusion.1 = (bf16[1,8,128,1024]{3,2,0,1:T(8,128)(2,1)}, bf16[1,8,128,1024]{3,2,0,1:T(8,128)(2,1)S(1)}) fusion(bf16[2,8,128,1024]{3,2,0,1:T(8,128)(2,1)} %all-to-all-done, f32[]{:T(128)S(6)} %min_shard_map.3), kind=kLoop, calls=%fused_computation.8 | loop fusion | flops 6291456 | bytes 8388612 | tf_op jit(solution)/shard_map/convert_element_type | solution.py:72
  262.1 1.3 copy-done.5
  263.5 3.3 fusion.11
  266.7 2.1 fusion.1
  268.8 1.6 select_reduce_fusion.1
  276.4 1.8 fusion.92
  287.8 1.1 fusion.99
  288.9 5.5 %fusion.10 = f32[1024,256]{0,1:T(8,128)} fusion(bf16[1024,1024]{1,0:T(8,128)(2,1)} %bitcast.197, bf16[1,1,2,1024,256]{4,3,2,1,0:T(8,128)(2,1)S(1)} %copy-done), kind=kOutput, calls=%fused_computation.77 | convolution fusion | flops 1074003968 | bytes 5767168 | tf_op jit(solution)/shard_map/dot_general | solution.py:36
  294.5 2.1 fusion.3
  296.5 2.4 select_reduce_fusion.3
  299.6 1.3 select_subtract_fusion.19
  300.9 1.3 fusion.44
  307.2 1.8 fusion.78
  323.2 2.3 pad_maximum_fusion
  325.5 4.7 %all-to-all-start.1 = ((bf16[2,8,128,1024]{3,2,0,1:T(8,128)(2,1)}), bf16[2,8,128,1024]{3,2,0,1:T(8,128)(2,1)}, u32[]{:S(2)}, u32[]{:S(2)}) async-start(bf16[2,8,128,1024]{3,2,0,1:T(8,128)(2,1)} %pad_maximum_fusion), calls=%async_computation.2 | async-start | bytes 8388608 | tf_op jit(solution)/shard_map/all_to_all | solution.py:122
  331.6 1.3 fusion.101
  333.9 1.4 fusion.100
  336.4 1.1 maximum_bitcast_fusion
  337.4 85.5 %all-to-all-done.1 = bf16[2,8,128,1024]{3,2,0,1:T(8,128)(2,1)} async-done(((bf16[2,8,128,1024]{3,2,0,1:T(8,128)(2,1)}), bf16[2,8,128,1024]{3,2,0,1:T(8,128)(2,1)}, u32[]{:S(2)}, u32[]{:S(2)}) %all-to-all-start.1) | async-done | bytes 4194336 | tf_op jit(solution)/shard_map/all_to_all | solution.py:122
  422.9 2.6 copy.32
  425.5 2.3 copy.29
  427.9 1.5 convolution_convert_fusion
  429.4 2.3 copy.30
  431.7 2.2 slice.20
  (110 shorter events, 35.7 us)
Async XLA Ops:
  7.2 120.1 %reduce-scatter.2.cloned.1.call-start = ((), (), s32[]{:S(2)}) async-start(), calls=%async_computation.3 | async-start | bytes 18350080 | tf_op jit(solution)/shard_map/reduce_scatter | solution.py:89
  7.2 0.7 copy-start.18
  137.6 119.5 %all-to-all-start = ((bf16[2,8,128,1024]{3,2,0,1:T(8,128)(2,1)}), bf16[2,8,128,1024]{3,2,0,1:T(8,128)(2,1)}, u32[]{:S(2)}, u32[]{:S(2)}) async-start(bf16[2,8,128,1024]{3,2,0,1:T(8,128)(2,1)} %copy.20), calls=%async_computation.1 | async-start | bytes 8388608 | tf_op jit(solution)/shard_map/all_to_all | solution.py:113
  257.1 6.3 %copy-start = (bf16[1,1,2,1024,256]{4,3,2,1,0:T(8,128)(2,1)S(1)}, bf16[1,1,2,1024,256]{4,3,2,1,0:T(8,128)(2,1)}, u32[]{:S(2)}) copy-start(bf16[1,1,2,1024,256]{4,3,2,1,0:T(8,128)(2,1)} %param.4) | copy-start | bytes 3145732
  262.1 1.3 copy-start.5
  274.4 4.1 copy-start.6
  279.6 0.8 copy-start.8
  281.7 5.7 %copy-start.16 = (f32[256,256]{1,0:T(8,128)}, f32[256,256]{1,0:T(8,128)S(1)}, u32[]{:S(2)}) copy-start(f32[256,256]{1,0:T(8,128)S(1)} %get-tuple-element.9) | copy-start | bytes 786436
  304.8 4.5 %copy-start.3 = (bf16[1,8,128,1024]{3,2,0,1:T(8,128)(2,1)S(1)}, bf16[1,8,128,1024]{3,2,0,1:T(8,128)(2,1)}, u32[]{:S(2)}) copy-start(bf16[1,8,128,1024]{3,2,0,1:T(8,128)(2,1)} %get-tuple-element.4) | copy-start | bytes 6291460
  309.0 1.5 copy-start.1
  310.2 1.4 copy-start.10
  311.5 5.5 %copy-start.17 = (f32[256,256]{1,0:T(8,128)}, f32[256,256]{1,0:T(8,128)S(1)}, u32[]{:S(2)}) copy-start(f32[256,256]{1,0:T(8,128)S(1)} %get-tuple-element.13) | copy-start | bytes 786436
  313.1 4.8 %copy-start.12 = (f32[256,256]{1,0:T(8,128)S(1)}, f32[256,256]{1,0:T(8,128)}, u32[]{:S(2)}) copy-start(f32[256,256]{1,0:T(8,128)} %fusion.99) | copy-start | bytes 786436
  314.7 4.6 %copy-start.9 = (bf16[1024,256]{1,0:T(8,128)(2,1)S(1)}, bf16[1024,256]{1,0:T(8,128)(2,1)}, u32[]{:S(2)}) copy-start(bf16[1024,256]{1,0:T(8,128)(2,1)} %copy-done.8) | copy-start | bytes 1572868
  315.1 4.9 %copy-start.7 = (bf16[1,8,128,1024]{3,2,0,1:T(8,128)(2,1)S(1)}, bf16[1,8,128,1024]{3,2,0,1:T(8,128)(2,1)}, u32[]{:S(2)}) copy-start(bf16[1,8,128,1024]{3,2,0,1:T(8,128)(2,1)} %copy-done.5) | copy-start | bytes 6291460
  318.7 0.7 copy-start.13
  319.4 2.2 copy-start.11
  320.0 2.4 copy-start.2
  320.0 2.4 copy-start.4
  321.6 1.6 copy-start.15
  325.5 6.1 %copy-start.14 = (f32[256,256]{1,0:T(8,128)S(1)}, f32[256,256]{1,0:T(8,128)}, u32[]{:S(2)}) copy-start(f32[256,256]{1,0:T(8,128)} %copy-done.13) | copy-start | bytes 786436
  325.5 97.4 %all-to-all-start.1 = ((bf16[2,8,128,1024]{3,2,0,1:T(8,128)(2,1)}), bf16[2,8,128,1024]{3,2,0,1:T(8,128)(2,1)}, u32[]{:S(2)}, u32[]{:S(2)}) async-start(bf16[2,8,128,1024]{3,2,0,1:T(8,128)(2,1)} %pad_maximum_fusion), calls=%async_computation.2 | async-start | bytes 8388608 | tf_op jit(solution)/shard_map/all_to_all | solution.py:122
Sparse Core Ops, SparseCore 0:
  10.6 116.6 reduce-scatter.1
where the time goes:
time: 448 us; the launch traced here: 441 us
  waiting for transfers between devices  205 us (46%)
  blocking collectives  109 us (24%)
  matrix products  62.1 us (14%)
  local copies, waits for them, and re-layouts  21.7 us (5%)
  between operations  19.8 us (4%)
  other arithmetic  13.8 us (3%)
  starting transfers between devices  10.2 us (2%)
    reduce_scatter x1, waiting for transfers between devices, local(): lax.psum_scatter(partials[0].astype(jnp.float32).astype(jnp.bfloat16), 'r...  118 us
    psum x1, blocking collectives, local(): sum_squares = lax.psum(squared_sum(reduced), ('fsdp', 'rep'))  109 us
    all_to_all x1, waiting for transfers between devices, local(): lax.all_to_all(stacked, 'fsdp', split_axis=1, concat_axis=1, tiled=True)  85.5 us
    unnamed x42, local copies, waits for them, and re-layouts  12.5 us
    dot_general x20, matrix products, inverse_root(): jnp.dot(inverse, current, precision=lax.Precision.HIGHEST)  9.95 us
    dot_general x16, matrix products, inverse_root(): current = jnp.dot(current, middle, precision=lax.Precision.HIGHEST)  8.99 us
  transfers between devices with their start and end apart: 3, of which 2 were waited for; matrix products, arithmetic and copies ran while one was open for 3% of the time, Pallas kernels for 0%

commit v1 on v0

--- a/solution.py
+++ b/solution.py
@@ -104,7 +104,7 @@
     flattened = reduced.reshape(per_slice, row_count * block_width)
     outgoing = jnp.dot(selector, flattened, preferred_element_type=jnp.float32).astype(jnp.bfloat16)
     outgoing = outgoing.reshape(slot_count, fsdp_count, row_count, block_width)
-    sum_squares = lax.psum(squared_sum(reduced), ("fsdp", "rep"))
+    sum_squares = lax.psum(lax.psum(squared_sum(reduced), "rep"), "fsdp")
     clip_limit = 0.5 * math.sqrt(block_total * block_width * block_width)
     clip_factor = jnp.minimum(1.0, clip_limit / jnp.sqrt(sum_squares + 1e-06))
     filled = jnp.sum((my_owners == lax.axis_index("fsdp")).astype(jnp.int32))

time: 448 us -> 434 us (0.969)
  blocking collectives: 109 us -> 80.9 us
  starting transfers between devices: 10.2 us -> 18.8 us
  waiting for transfers between devices: 205 us -> 210 us
    psum x1 -> x2, blocking collectives: 109 us -> 80.9 us  [local(): sum_squares = lax.psum(lax.psum(squared_sum(reduced), 'rep'), 'fsdp')]
    all_to_all x1, starting transfers between devices: 4.67 us -> 13.3 us  [local(): lax.all_to_all(stacked, 'fsdp', split_axis=1, concat_axis=1, tiled=True)]
    all_to_all x1, waiting for transfers between devices: 0.01 us -> 7.04 us  [local(): lax.all_to_all(outgoing, 'fsdp', split_axis=1, concat_axis=1, tiled=True)]
  transfers between devices with their start and end apart: 3 -> 3, of which waited for: 2 -> 3; matrix products, arithmetic and copies ran while one was open for 3% -> 3% of each run, Pallas kernels for 0% -> 0%
where the time goes in v1:
time: 434 us; the launch traced here: 427 us
  waiting for transfers between devices  210 us (48%)
  blocking collectives  80.9 us (19%)
  matrix products  62.3 us (14%)
  local copies, waits for them, and re-layouts  21.5 us (5%)
  between operations  19.9 us (5%)
  starting transfers between devices  18.8 us (4%)
  other arithmetic  13.6 us (3%)
    reduce_scatter x1, waiting for transfers between devices, local(): lax.psum_scatter(partials[0].astype(jnp.float32).astype(jnp.bfloat16), 'r...  119 us
    all_to_all x1, waiting for transfers between devices, local(): lax.all_to_all(stacked, 'fsdp', split_axis=1, concat_axis=1, tiled=True)  83.5 us
    psum x2, blocking collectives, local(): sum_squares = lax.psum(lax.psum(squared_sum(reduced), 'rep'), 'fsdp')  80.9 us
    all_to_all x1, starting transfers between devices, local(): lax.all_to_all(stacked, 'fsdp', split_axis=1, concat_axis=1, tiled=True)  13.3 us
    unnamed x42, local copies, waits for them, and re-layouts  12.4 us
    dot_general x20, matrix products, inverse_root(): jnp.dot(inverse, current, precision=lax.Precision.HIGHEST)  10 us
    dot_general x16, matrix products, inverse_root(): current = jnp.dot(current, middle, precision=lax.Precision.HIGHEST)  9.07 us
    dot_general x2, matrix products, precondition(): jnp.dot(gradient, projected, preferred_element_type=jnp.float32)  8.78 us
  transfers between devices with their start and end apart: 3, of which 3 were waited for; matrix products, arithmetic and copies ran while one was open for 3% of the time, Pallas kernels for 0%

profile of v1, /device:TPU:0, one launch (start us, length us, event | category | flops | bytes accessed | tf_op | source)
XLA Modules:
  0.0 426.8 jit_solution(8475079314243421791)
XLA Ops:
  8.7 118.5 %reduce-scatter.2.cloned.1.call-done = bf16[14,128,1024]{2,1,0:T(8,128)(2,1)} async-done(((bf16[56,128,1024]{2,1,0:T(8,128)(2,1)}), bf16[14,128,1024]{2,1,0:T(8,128)(2,1)}) %reduce-scatter.2.cloned.1.call-update) | async-done | bytes 3670032 | tf_op jit(solution)/shard_map/reduce_scatter | solution.py:89
  127.3 2.5 pad.4
  129.8 2.3 copy.28
  132.1 1.2 convolution_convert_fusion.1
  133.3 4.3 %copy.20 = bf16[2,8,128,1024]{3,2,0,1:T(8,128)(2,1)} copy(bf16[2,8,128,1024]{3,1,2,0:T(8,128)(2,1)S(1)} %bitcast.193) | data formatting | bytes 8388608 | tf_op jit(solution)/shard_map/reshape | solution.py:106
  137.6 5.5 %all-to-all-start = ((bf16[2,8,128,1024]{3,2,0,1:T(8,128)(2,1)}), bf16[2,8,128,1024]{3,2,0,1:T(8,128)(2,1)}, u32[]{:S(2)}, u32[]{:S(2)}) async-start(bf16[2,8,128,1024]{3,2,0,1:T(8,128)(2,1)} %copy.20), calls=%async_computation.1 | async-start | bytes 8388608 | tf_op jit(solution)/shard_map/all_to_all | solution.py:113
  143.1 4.5 %multiply_reduce_fusion = f32[]{:T(128)} fusion(bf16[14,128,1024]{2,1,0:T(8,128)(2,1)} %reduce-scatter.2.cloned.1.call-done), kind=kLoop, calls=%fused_computation.2 | loop fusion | flops 5505023 | bytes 3670020 | tf_op jit(solution)/shard_map/reduce_sum | solution.py:67
  147.7 6.7 %psum.14 = f32[]{:T(128)} all-reduce(f32[]{:T(128)} %multiply_reduce_fusion), channel_id=1, replica_groups=mesh['fsdp'=8,'rep'=4] {'rep'}, use_global_device_ids=true, to_apply=%region_3.0 | all-reduce | flops 1 | bytes 8 | tf_op jit(solution)/shard_map/psum | solution.py:107
  154.3 74.3 %psum.15 = f32[]{:T(128)} all-reduce(f32[]{:T(128)} %psum.14), channel_id=1, replica_groups=mesh['fsdp'=8,'rep'=4] {'fsdp'}, use_global_device_ids=true, to_apply=%region_4.0 | all-reduce | flops 1 | bytes 8 | tf_op jit(solution)/shard_map/psum | solution.py:107
  229.3 7.0 %all-to-all-done = bf16[2,8,128,1024]{3,2,0,1:T(8,128)(2,1)} async-done(((bf16[2,8,128,1024]{3,2,0,1:T(8,128)(2,1)}), bf16[2,8,128,1024]{3,2,0,1:T(8,128)(2,1)}, u32[]{:S(2)}, u32[]{:S(2)}) %all-to-all-start) | async-done | bytes 4194336 | tf_op jit(solution)/shard_map/all_to_all | solution.py:113
  236.3 4.9 %multiply_convert_fusion.1 = (bf16[1,8,128,1024]{3,2,0,1:T(8,128)(2,1)}, bf16[1,8,128,1024]{3,2,0,1:T(8,128)(2,1)S(1)}) fusion(bf16[2,8,128,1024]{3,2,0,1:T(8,128)(2,1)} %all-to-all-done, f32[]{:T(128)S(6)} %min_shard_map.3), kind=kLoop, calls=%fused_computation.8 | loop fusion | flops 6291456 | bytes 8388612 | tf_op jit(solution)/shard_map/convert_element_type | solution.py:72
  241.2 1.3 copy-done.5
  242.5 3.3 fusion.11
  245.8 2.1 fusion.1
  247.9 1.6 select_reduce_fusion.1
  255.5 1.8 fusion.92
  268.0 5.5 %fusion.10 = f32[1024,256]{0,1:T(8,128)} fusion(bf16[1024,1024]{1,0:T(8,128)(2,1)} %bitcast.197, bf16[1,1,2,1024,256]{4,3,2,1,0:T(8,128)(2,1)S(1)} %copy-done), kind=kOutput, calls=%fused_computation.77 | convolution fusion | flops 1074003968 | bytes 5767168 | tf_op jit(solution)/shard_map/dot_general | solution.py:36
  273.5 2.1 fusion.3
  275.6 2.4 select_reduce_fusion.3
  278.7 1.3 select_subtract_fusion.19
  280.0 1.3 fusion.44
  286.3 1.8 fusion.78
  302.6 2.3 pad_maximum_fusion
  304.9 13.3 %all-to-all-start.1 = ((bf16[2,8,128,1024]{3,2,0,1:T(8,128)(2,1)}), bf16[2,8,128,1024]{3,2,0,1:T(8,128)(2,1)}, u32[]{:S(2)}, u32[]{:S(2)}) async-start(bf16[2,8,128,1024]{3,2,0,1:T(8,128)(2,1)} %pad_maximum_fusion), calls=%async_computation.2 | async-start | bytes 8388608 | tf_op jit(solution)/shard_map/all_to_all | solution.py:122
  319.4 1.3 fusion.101
  321.7 1.4 fusion.100
  325.2 83.5 %all-to-all-done.1 = bf16[2,8,128,1024]{3,2,0,1:T(8,128)(2,1)} async-done(((bf16[2,8,128,1024]{3,2,0,1:T(8,128)(2,1)}), bf16[2,8,128,1024]{3,2,0,1:T(8,128)(2,1)}, u32[]{:S(2)}, u32[]{:S(2)}) %all-to-all-start.1) | async-done | bytes 4194336 | tf_op jit(solution)/shard_map/all_to_all | solution.py:122
  408.7 2.6 copy.32
  411.4 2.3 copy.29
  413.7 1.5 convolution_convert_fusion
  415.2 2.3 copy.30
  417.6 2.2 slice.20
  (111 shorter events, 37.8 us)
Async XLA Ops:
  7.2 120.1 %reduce-scatter.2.cloned.1.call-start = ((), (), s32[]{:S(2)}) async-start(), calls=%async_computation.3 | async-start | bytes 18350080 | tf_op jit(solution)/shard_map/reduce_scatter | solution.py:89
  7.2 0.7 copy-start.18
  137.6 98.7 %all-to-all-start = ((bf16[2,8,128,1024]{3,2,0,1:T(8,128)(2,1)}), bf16[2,8,128,1024]{3,2,0,1:T(8,128)(2,1)}, u32[]{:S(2)}, u32[]{:S(2)}) async-start(bf16[2,8,128,1024]{3,2,0,1:T(8,128)(2,1)} %copy.20), calls=%async_computation.1 | async-start | bytes 8388608 | tf_op jit(solution)/shard_map/all_to_all | solution.py:113
  229.3 13.2 %copy-start = (bf16[1,1,2,1024,256]{4,3,2,1,0:T(8,128)(2,1)S(1)}, bf16[1,1,2,1024,256]{4,3,2,1,0:T(8,128)(2,1)}, u32[]{:S(2)}) copy-start(bf16[1,1,2,1024,256]{4,3,2,1,0:T(8,128)(2,1)} %param.4) | copy-start | bytes 3145732
  241.2 1.3 copy-start.5
  253.5 4.1 copy-start.6
  258.7 0.8 copy-start.8
  260.8 5.7 %copy-start.16 = (f32[256,256]{1,0:T(8,128)}, f32[256,256]{1,0:T(8,128)S(1)}, u32[]{:S(2)}) copy-start(f32[256,256]{1,0:T(8,128)S(1)} %get-tuple-element.9) | copy-start | bytes 786436
  284.0 4.5 %copy-start.3 = (bf16[1,8,128,1024]{3,2,0,1:T(8,128)(2,1)S(1)}, bf16[1,8,128,1024]{3,2,0,1:T(8,128)(2,1)}, u32[]{:S(2)}) copy-start(bf16[1,8,128,1024]{3,2,0,1:T(8,128)(2,1)} %get-tuple-element.4) | copy-start | bytes 6291460
  288.1 1.5 copy-start.1
  289.3 1.4 copy-start.10
  290.7 5.8 %copy-start.17 = (f32[256,256]{1,0:T(8,128)}, f32[256,256]{1,0:T(8,128)S(1)}, u32[]{:S(2)}) copy-start(f32[256,256]{1,0:T(8,128)S(1)} %get-tuple-element.13) | copy-start | bytes 786436
  292.4 4.9 %copy-start.12 = (f32[256,256]{1,0:T(8,128)S(1)}, f32[256,256]{1,0:T(8,128)}, u32[]{:S(2)}) copy-start(f32[256,256]{1,0:T(8,128)} %fusion.99) | copy-start | bytes 786436
  294.1 4.6 %copy-start.9 = (bf16[1024,256]{1,0:T(8,128)(2,1)S(1)}, bf16[1024,256]{1,0:T(8,128)(2,1)}, u32[]{:S(2)}) copy-start(bf16[1024,256]{1,0:T(8,128)(2,1)} %copy-done.8) | copy-start | bytes 1572868
  294.5 4.9 %copy-start.7 = (bf16[1,8,128,1024]{3,2,0,1:T(8,128)(2,1)S(1)}, bf16[1,8,128,1024]{3,2,0,1:T(8,128)(2,1)}, u32[]{:S(2)}) copy-start(bf16[1,8,128,1024]{3,2,0,1:T(8,128)(2,1)} %copy-done.5) | copy-start | bytes 6291460
  298.0 0.7 copy-start.13
  298.7 2.2 copy-start.11
  299.4 2.4 copy-start.2
  299.4 2.4 copy-start.4
  301.0 1.6 copy-start.15
  304.9 14.5 %copy-start.14 = (f32[256,256]{1,0:T(8,128)S(1)}, f32[256,256]{1,0:T(8,128)}, u32[]{:S(2)}) copy-start(f32[256,256]{1,0:T(8,128)} %copy-done.13) | copy-start | bytes 786436
  304.9 103.8 %all-to-all-start.1 = ((bf16[2,8,128,1024]{3,2,0,1:T(8,128)(2,1)}), bf16[2,8,128,1024]{3,2,0,1:T(8,128)(2,1)}, u32[]{:S(2)}, u32[]{:S(2)}) async-start(bf16[2,8,128,1024]{3,2,0,1:T(8,128)(2,1)} %pad_maximum_fusion), calls=%async_computation.2 | async-start | bytes 8388608 | tf_op jit(solution)/shard_map/all_to_all | solution.py:122
Sparse Core Ops, SparseCore 0:
  10.6 116.6 reduce-scatter.1
